TPU v7x, 128 devices: a whole 4x4x4 slice. The times are simulated.
128 devices in a mesh: dp: 1, ep: 128 (over z, y, x, core).
Axes of the slice: x: 4, y: 4, z: 4, core: 2. Of those that a mesh axis runs over, the one named last changes fastest.
Arguments:
- tokens: bfloat16 [65536, 1024], P(('dp', 'ep'))
- slot_ids: int32 [65536, 4, 32], P(('dp', 'ep'))
- request_rows: int32 [128, 128, 64], P(('dp', 'ep'))
- gate_vals: float32 [65536, 4, 32], P(('dp', 'ep'))
- grad_out: bfloat16 [65536, 1024], P(('dp', 'ep'))
- table_up: bfloat16 [16384, 1024], P('ep')
- table_down: bfloat16 [16384, 1024], P('ep')
Outputs:
- output 1: bfloat16 [65536, 1024], P(('dp', 'ep'))
- output 2: bfloat16 [65536, 1024], P(('dp', 'ep'))
- output 3: bfloat16 [16384, 1024], P(('dp', 'ep'))
- output 4: bfloat16 [16384, 1024], P(('dp', 'ep'))
All inputs are finite; a program needn't handle non-finite values.
Results may differ from a plain program's by a relative error of at most 0.00849675.
Values are sent between devices in bfloat16 or wider.
A program may use at most 1 GiB of HBM per device.

v0:
```python
import math
import jax
import jax.numpy as jnp
from jax import lax
from jax.sharding import PartitionSpec as P


def gelu_pair(pre_act):
    normal_cdf = 0.5 * (1.0 + lax.erf(pre_act * (2.0 ** -0.5)))
    normal_pdf = jnp.exp(-0.5 * pre_act * pre_act) * ((2.0 * math.pi) ** -0.5)
    return pre_act * normal_cdf, normal_cdf + pre_act * normal_pdf


def local_layer(tokens, slot_flat, gate_flat, grad_out, up_table, down_table):
    tok_dev, width = tokens.shape
    sel_tok = slot_flat.shape[1]
    n_slots = up_table.shape[0]
    cap_tokens = max(1, 2 ** 23 // (sel_tok * width))
    block_tok = math.gcd(tok_dev, 2 ** int(math.log2(cap_tokens)))
    n_blocks = tok_dev // block_tok

    def scan_step(acc_pair, block_in):
        acc_up, acc_down = acc_pair
        x_blk, slot_blk, gate_blk, dy_blk = block_in
        up_rows = up_table[slot_blk]
        down_rows = down_table[slot_blk]
        pre_act = jnp.einsum('bsd,bd->bs', up_rows, x_blk, preferred_element_type=jnp.float32)
        act_val, slope_val = gelu_pair(pre_act)
        w_out = (gate_blk * act_val).astype(jnp.bfloat16)
        y_blk = jnp.einsum('bs,bsd->bd', w_out, down_rows, preferred_element_type=jnp.float32).astype(jnp.bfloat16)
        back_dot = jnp.einsum('bsd,bd->bs', down_rows, dy_blk, preferred_element_type=jnp.float32)
        coef_bf = (gate_blk * slope_val * back_dot).astype(jnp.bfloat16)
        dx_blk = jnp.einsum('bs,bsd->bd', coef_bf, up_rows, preferred_element_type=jnp.float32).astype(jnp.bfloat16)
        flat_slots = slot_blk.reshape(-1)
        up_part = coef_bf.astype(jnp.float32)[:, :, None] * x_blk[:, None, :]
        down_part = w_out.astype(jnp.float32)[:, :, None] * dy_blk[:, None, :]
        acc_up = acc_up.at[flat_slots].add(up_part.reshape(-1, width))
        acc_down = acc_down.at[flat_slots].add(down_part.reshape(-1, width))
        return (acc_up, acc_down), (y_blk, dx_blk)

    zero_acc = jnp.zeros((n_slots, width), jnp.float32)
    blocks_in = (tokens.reshape(n_blocks, block_tok, width), slot_flat.reshape(n_blocks, block_tok, sel_tok), gate_flat.reshape(n_blocks, block_tok, sel_tok), grad_out.reshape(n_blocks, block_tok, width))
    (acc_up, acc_down), (y_all, dx_all) = lax.scan(scan_step, (zero_acc, zero_acc), blocks_in)
    return acc_up, acc_down, y_all.reshape(tok_dev, width), dx_all.reshape(tok_dev, width)


def solution(mesh):
    n_group = mesh.shape['ep']
    tok_spec = P(('dp', 'ep'))
    table_spec = P('ep')

    def per_device(tokens, slot_ids, request_rows, gate_vals, grad_out, up_local, down_local):
        tok_dev, width = tokens.shape
        rows_owner = up_local.shape[0]
        n_req = request_rows.shape[2]
        sel_tok = slot_ids.shape[1] * slot_ids.shape[2]
        asked_rows = lax.all_to_all(request_rows[0], 'ep', 0, 0, tiled=True)
        up_pulled = lax.all_to_all(up_local[asked_rows], 'ep', 0, 0, tiled=True).reshape(n_group * n_req, width)
        down_pulled = lax.all_to_all(down_local[asked_rows], 'ep', 0, 0, tiled=True).reshape(n_group * n_req, width)
        acc_up, acc_down, y_local, dx_local = local_layer(tokens, slot_ids.reshape(tok_dev, sel_tok), gate_vals.reshape(tok_dev, sel_tok), grad_out, up_pulled, down_pulled)
        back_up = lax.all_to_all(acc_up.astype(jnp.bfloat16).reshape(n_group, n_req, width), 'ep', 0, 0, tiled=True)
        back_down = lax.all_to_all(acc_down.astype(jnp.bfloat16).reshape(n_group, n_req, width), 'ep', 0, 0, tiled=True)
        flat_asked = asked_rows.reshape(-1)
        grad_up = jax.ops.segment_sum(back_up.reshape(-1, width).astype(jnp.float32), flat_asked, num_segments=rows_owner)
        grad_down = jax.ops.segment_sum(back_down.reshape(-1, width).astype(jnp.float32), flat_asked, num_segments=rows_owner)
        return y_local, dx_local, grad_up.astype(jnp.bfloat16), grad_down.astype(jnp.bfloat16)

    return jax.shard_map(per_device, mesh=mesh, in_specs=(tok_spec, tok_spec, tok_spec, tok_spec, tok_spec, table_spec, table_spec), out_specs=(tok_spec, tok_spec, tok_spec, tok_spec), check_vma=False)
```

profile of v0, /device:TPU:11, one launch (start us, length us, event | category | flops | bytes accessed | tf_op | source)
XLA Modules:
  0.0 3825.0 jit_solution(10892038173642127904)
XLA Ops:
  1.5 18.3 all_to_all.32
  20.5 35.5 gather_fusion.3
  63.6 35.5 gather_fusion.2
  99.1 194.5 %all-to-all-done.2 = bf16[128,64,1024]{2,1,0:T(8,128)(2,1)} async-done(((bf16[128,64,1024]{2,1,0:T(8,128)(2,1)}), bf16[128,64,1024]{2,1,0:T(8,128)(2,1)}, u32[]{:S(2)}, u32[]{:S(2)}) %all-to-all-start.2) | async-done | bytes 16777248 | tf_op jit(solution)/shard_map/all_to_all | solution.py:59
  293.6 19.9 all-to-all-start.1
  315.0 228.5 %all-to-all-done.1 = bf16[128,64,1024]{2,1,0:T(8,128)(2,1)} async-done(((bf16[128,64,1024]{2,1,0:T(8,128)(2,1)}), bf16[128,64,1024]{2,1,0:T(8,128)(2,1)}, u32[]{:S(2)}, u32[]{:S(2)}) %all-to-all-start.1) | async-done | bytes 16777248 | tf_op jit(solution)/shard_map/all_to_all | solution.py:58
  543.5 11.3 broadcast_in_dim.8.clone
  554.8 11.3 broadcast_in_dim.8
  566.1 2672.2 %while.16 = (s32[]{:T(128)}, f32[8192,1024]{1,0:T(8,128)}, f32[8192,1024]{1,0:T(8,128)}, bf16[8,64,1024]{2,1,0:T(8,128)(2,1)}, bf16[8,64,1024]{2,1,0:T(8,128)(2,...) while((s32[]{:T(128)}, f32[8192,1024]{1,0:T(8,128)}, ...), condition=%wide.region_3.4_spmd, body=%wide.region_0.3_spmd.sunk | while | flops 100982784 | bytes 458359104 | solution.py:43
  568.8 48.6 %gather_fusion.1 = bf16[8192,1024]{1,0:T(8,128)(2,1)} fusion(bf16[8192,1024]{1,0:T(8,128)(2,1)} %get-tuple-element.256, s32[8192]{0:T(1024)S(1)} %get-tuple-element.211), kind=kCustom, calls=%fused_computation.1.clone.1 | custom fusion | bytes 33587200 | tf_op jit(solution)/shard_map/while/body/eval_jaxpr/gather | solution.py:26
  625.5 48.7 %gather_fusion = bf16[8192,1024]{1,0:T(8,128)(2,1)} fusion(bf16[8192,1024]{1,0:T(8,128)(2,1)} %get-tuple-element.254, s32[8192]{0:T(1024)S(1)} %get-tuple-element.211), kind=kCustom, calls=%fused_computation.clone.1 | custom fusion | bytes 33587200 | tf_op jit(solution)/shard_map/while/body/eval_jaxpr/gather | solution.py:25
  682.4 8.2 fusion.60
  693.7 21.4 bitcast_multiply_fusion.4
  715.1 92.5 %scatter_fusion = f32[8192,1024]{1,0:T(8,128)} fusion(f32[8192,1024]{1,0:T(8,128)} %get-tuple-element.236, s32[8192]{0:T(1024)S(1)} %bitcast.137, f32[8192,1024]{1,0:T(8,128)} %get-tuple-element.217), kind=kCustom, calls=%fused_computation.4.clone.1 | custom fusion | flops 8388608 | bytes 100696064 | tf_op jit(solution)/shard_map/while/body/eval_jaxpr/scatter-add | solution.py:37
  807.6 92.5 %scatter_fusion.1 = f32[8192,1024]{1,0:T(8,128)} fusion(f32[8192,1024]{1,0:T(8,128)} %get-tuple-element.237, s32[8192]{0:T(1024)S(1)} %bitcast.138, f32[8192,1024]{1,0:T(8,128)} %get-tuple-element.218), kind=kCustom, calls=%fused_computation.5.clone.1 | custom fusion | flops 8388608 | bytes 100696064 | tf_op jit(solution)/shard_map/while/body/eval_jaxpr/scatter-add | solution.py:38
  902.8 48.6 %gather_fusion.1 = bf16[8192,1024]{1,0:T(8,128)(2,1)} fusion(bf16[8192,1024]{1,0:T(8,128)(2,1)} %get-tuple-element.256, s32[8192]{0:T(1024)S(1)} %get-tuple-element.211), kind=kCustom, calls=%fused_computation.1.clone.1 | custom fusion | bytes 33587200 | tf_op jit(solution)/shard_map/while/body/eval_jaxpr/gather | solution.py:26
  959.5 48.7 %gather_fusion = bf16[8192,1024]{1,0:T(8,128)(2,1)} fusion(bf16[8192,1024]{1,0:T(8,128)(2,1)} %get-tuple-element.254, s32[8192]{0:T(1024)S(1)} %get-tuple-element.211), kind=kCustom, calls=%fused_computation.clone.1 | custom fusion | bytes 33587200 | tf_op jit(solution)/shard_map/while/body/eval_jaxpr/gather | solution.py:25
  1016.4 8.2 fusion.60
  1027.7 21.4 bitcast_multiply_fusion.4
  1049.1 92.5 %scatter_fusion = f32[8192,1024]{1,0:T(8,128)} fusion(f32[8192,1024]{1,0:T(8,128)} %get-tuple-element.236, s32[8192]{0:T(1024)S(1)} %bitcast.137, f32[8192,1024]{1,0:T(8,128)} %get-tuple-element.217), kind=kCustom, calls=%fused_computation.4.clone.1 | custom fusion | flops 8388608 | bytes 100696064 | tf_op jit(solution)/shard_map/while/body/eval_jaxpr/scatter-add | solution.py:37
  1141.6 92.5 %scatter_fusion.1 = f32[8192,1024]{1,0:T(8,128)} fusion(f32[8192,1024]{1,0:T(8,128)} %get-tuple-element.237, s32[8192]{0:T(1024)S(1)} %bitcast.138, f32[8192,1024]{1,0:T(8,128)} %get-tuple-element.218), kind=kCustom, calls=%fused_computation.5.clone.1 | custom fusion | flops 8388608 | bytes 100696064 | tf_op jit(solution)/shard_map/while/body/eval_jaxpr/scatter-add | solution.py:38
  1236.9 48.6 %gather_fusion.1 = bf16[8192,1024]{1,0:T(8,128)(2,1)} fusion(bf16[8192,1024]{1,0:T(8,128)(2,1)} %get-tuple-element.256, s32[8192]{0:T(1024)S(1)} %get-tuple-element.211), kind=kCustom, calls=%fused_computation.1.clone.1 | custom fusion | bytes 33587200 | tf_op jit(solution)/shard_map/while/body/eval_jaxpr/gather | solution.py:26
  1293.5 48.7 %gather_fusion = bf16[8192,1024]{1,0:T(8,128)(2,1)} fusion(bf16[8192,1024]{1,0:T(8,128)(2,1)} %get-tuple-element.254, s32[8192]{0:T(1024)S(1)} %get-tuple-element.211), kind=kCustom, calls=%fused_computation.clone.1 | custom fusion | bytes 33587200 | tf_op jit(solution)/shard_map/while/body/eval_jaxpr/gather | solution.py:25
  1350.4 8.2 fusion.60
  1361.8 21.4 bitcast_multiply_fusion.4
  1383.1 92.5 %scatter_fusion = f32[8192,1024]{1,0:T(8,128)} fusion(f32[8192,1024]{1,0:T(8,128)} %get-tuple-element.236, s32[8192]{0:T(1024)S(1)} %bitcast.137, f32[8192,1024]{1,0:T(8,128)} %get-tuple-element.217), kind=kCustom, calls=%fused_computation.4.clone.1 | custom fusion | flops 8388608 | bytes 100696064 | tf_op jit(solution)/shard_map/while/body/eval_jaxpr/scatter-add | solution.py:37
  1475.6 92.5 %scatter_fusion.1 = f32[8192,1024]{1,0:T(8,128)} fusion(f32[8192,1024]{1,0:T(8,128)} %get-tuple-element.237, s32[8192]{0:T(1024)S(1)} %bitcast.138, f32[8192,1024]{1,0:T(8,128)} %get-tuple-element.218), kind=kCustom, calls=%fused_computation.5.clone.1 | custom fusion | flops 8388608 | bytes 100696064 | tf_op jit(solution)/shard_map/while/body/eval_jaxpr/scatter-add | solution.py:38
  1570.9 48.6 %gather_fusion.1 = bf16[8192,1024]{1,0:T(8,128)(2,1)} fusion(bf16[8192,1024]{1,0:T(8,128)(2,1)} %get-tuple-element.256, s32[8192]{0:T(1024)S(1)} %get-tuple-element.211), kind=kCustom, calls=%fused_computation.1.clone.1 | custom fusion | bytes 33587200 | tf_op jit(solution)/shard_map/while/body/eval_jaxpr/gather | solution.py:26
  1627.6 48.7 %gather_fusion = bf16[8192,1024]{1,0:T(8,128)(2,1)} fusion(bf16[8192,1024]{1,0:T(8,128)(2,1)} %get-tuple-element.254, s32[8192]{0:T(1024)S(1)} %get-tuple-element.211), kind=kCustom, calls=%fused_computation.clone.1 | custom fusion | bytes 33587200 | tf_op jit(solution)/shard_map/while/body/eval_jaxpr/gather | solution.py:25
  1684.4 8.2 fusion.60
  1695.8 21.4 bitcast_multiply_fusion.4
  1717.2 92.5 %scatter_fusion = f32[8192,1024]{1,0:T(8,128)} fusion(f32[8192,1024]{1,0:T(8,128)} %get-tuple-element.236, s32[8192]{0:T(1024)S(1)} %bitcast.137, f32[8192,1024]{1,0:T(8,128)} %get-tuple-element.217), kind=kCustom, calls=%fused_computation.4.clone.1 | custom fusion | flops 8388608 | bytes 100696064 | tf_op jit(solution)/shard_map/while/body/eval_jaxpr/scatter-add | solution.py:37
  1809.7 92.5 %scatter_fusion.1 = f32[8192,1024]{1,0:T(8,128)} fusion(f32[8192,1024]{1,0:T(8,128)} %get-tuple-element.237, s32[8192]{0:T(1024)S(1)} %bitcast.138, f32[8192,1024]{1,0:T(8,128)} %get-tuple-element.218), kind=kCustom, calls=%fused_computation.5.clone.1 | custom fusion | flops 8388608 | bytes 100696064 | tf_op jit(solution)/shard_map/while/body/eval_jaxpr/scatter-add | solution.py:38
  1904.9 48.6 %gather_fusion.1 = bf16[8192,1024]{1,0:T(8,128)(2,1)} fusion(bf16[8192,1024]{1,0:T(8,128)(2,1)} %get-tuple-element.256, s32[8192]{0:T(1024)S(1)} %get-tuple-element.211), kind=kCustom, calls=%fused_computation.1.clone.1 | custom fusion | bytes 33587200 | tf_op jit(solution)/shard_map/while/body/eval_jaxpr/gather | solution.py:26
  1961.6 48.7 %gather_fusion = bf16[8192,1024]{1,0:T(8,128)(2,1)} fusion(bf16[8192,1024]{1,0:T(8,128)(2,1)} %get-tuple-element.254, s32[8192]{0:T(1024)S(1)} %get-tuple-element.211), kind=kCustom, calls=%fused_computation.clone.1 | custom fusion | bytes 33587200 | tf_op jit(solution)/shard_map/while/body/eval_jaxpr/gather | solution.py:25
  2018.5 8.2 fusion.60
  2029.8 21.4 bitcast_multiply_fusion.4
  2051.2 92.5 %scatter_fusion = f32[8192,1024]{1,0:T(8,128)} fusion(f32[8192,1024]{1,0:T(8,128)} %get-tuple-element.236, s32[8192]{0:T(1024)S(1)} %bitcast.137, f32[8192,1024]{1,0:T(8,128)} %get-tuple-element.217), kind=kCustom, calls=%fused_computation.4.clone.1 | custom fusion | flops 8388608 | bytes 100696064 | tf_op jit(solution)/shard_map/while/body/eval_jaxpr/scatter-add | solution.py:37
  2143.7 92.5 %scatter_fusion.1 = f32[8192,1024]{1,0:T(8,128)} fusion(f32[8192,1024]{1,0:T(8,128)} %get-tuple-element.237, s32[8192]{0:T(1024)S(1)} %bitcast.138, f32[8192,1024]{1,0:T(8,128)} %get-tuple-element.218), kind=kCustom, calls=%fused_computation.5.clone.1 | custom fusion | flops 8388608 | bytes 100696064 | tf_op jit(solution)/shard_map/while/body/eval_jaxpr/scatter-add | solution.py:38
  2238.9 48.6 %gather_fusion.1 = bf16[8192,1024]{1,0:T(8,128)(2,1)} fusion(bf16[8192,1024]{1,0:T(8,128)(2,1)} %get-tuple-element.256, s32[8192]{0:T(1024)S(1)} %get-tuple-element.211), kind=kCustom, calls=%fused_computation.1.clone.1 | custom fusion | bytes 33587200 | tf_op jit(solution)/shard_map/while/body/eval_jaxpr/gather | solution.py:26
  2295.6 48.7 %gather_fusion = bf16[8192,1024]{1,0:T(8,128)(2,1)} fusion(bf16[8192,1024]{1,0:T(8,128)(2,1)} %get-tuple-element.254, s32[8192]{0:T(1024)S(1)} %get-tuple-element.211), kind=kCustom, calls=%fused_computation.clone.1 | custom fusion | bytes 33587200 | tf_op jit(solution)/shard_map/while/body/eval_jaxpr/gather | solution.py:25
  2352.5 8.2 fusion.60
  2363.8 21.4 bitcast_multiply_fusion.4
  2385.2 92.5 %scatter_fusion = f32[8192,1024]{1,0:T(8,128)} fusion(f32[8192,1024]{1,0:T(8,128)} %get-tuple-element.236, s32[8192]{0:T(1024)S(1)} %bitcast.137, f32[8192,1024]{1,0:T(8,128)} %get-tuple-element.217), kind=kCustom, calls=%fused_computation.4.clone.1 | custom fusion | flops 8388608 | bytes 100696064 | tf_op jit(solution)/shard_map/while/body/eval_jaxpr/scatter-add | solution.py:37
  2477.7 92.5 %scatter_fusion.1 = f32[8192,1024]{1,0:T(8,128)} fusion(f32[8192,1024]{1,0:T(8,128)} %get-tuple-element.237, s32[8192]{0:T(1024)S(1)} %bitcast.138, f32[8192,1024]{1,0:T(8,128)} %get-tuple-element.218), kind=kCustom, calls=%fused_computation.5.clone.1 | custom fusion | flops 8388608 | bytes 100696064 | tf_op jit(solution)/shard_map/while/body/eval_jaxpr/scatter-add | solution.py:38
  2573.0 48.6 %gather_fusion.1 = bf16[8192,1024]{1,0:T(8,128)(2,1)} fusion(bf16[8192,1024]{1,0:T(8,128)(2,1)} %get-tuple-element.256, s32[8192]{0:T(1024)S(1)} %get-tuple-element.211), kind=kCustom, calls=%fused_computation.1.clone.1 | custom fusion | bytes 33587200 | tf_op jit(solution)/shard_map/while/body/eval_jaxpr/gather | solution.py:26
  2629.6 48.7 %gather_fusion = bf16[8192,1024]{1,0:T(8,128)(2,1)} fusion(bf16[8192,1024]{1,0:T(8,128)(2,1)} %get-tuple-element.254, s32[8192]{0:T(1024)S(1)} %get-tuple-element.211), kind=kCustom, calls=%fused_computation.clone.1 | custom fusion | bytes 33587200 | tf_op jit(solution)/shard_map/while/body/eval_jaxpr/gather | solution.py:25
  2686.5 8.2 fusion.60
  2697.9 21.4 bitcast_multiply_fusion.4
  2719.3 92.5 %scatter_fusion = f32[8192,1024]{1,0:T(8,128)} fusion(f32[8192,1024]{1,0:T(8,128)} %get-tuple-element.236, s32[8192]{0:T(1024)S(1)} %bitcast.137, f32[8192,1024]{1,0:T(8,128)} %get-tuple-element.217), kind=kCustom, calls=%fused_computation.4.clone.1 | custom fusion | flops 8388608 | bytes 100696064 | tf_op jit(solution)/shard_map/while/body/eval_jaxpr/scatter-add | solution.py:37
  2811.8 92.5 %scatter_fusion.1 = f32[8192,1024]{1,0:T(8,128)} fusion(f32[8192,1024]{1,0:T(8,128)} %get-tuple-element.237, s32[8192]{0:T(1024)S(1)} %bitcast.138, f32[8192,1024]{1,0:T(8,128)} %get-tuple-element.218), kind=kCustom, calls=%fused_computation.5.clone.1 | custom fusion | flops 8388608 | bytes 100696064 | tf_op jit(solution)/shard_map/while/body/eval_jaxpr/scatter-add | solution.py:38
  2907.0 48.6 %gather_fusion.1 = bf16[8192,1024]{1,0:T(8,128)(2,1)} fusion(bf16[8192,1024]{1,0:T(8,128)(2,1)} %get-tuple-element.256, s32[8192]{0:T(1024)S(1)} %get-tuple-element.211), kind=kCustom, calls=%fused_computation.1.clone.1 | custom fusion | bytes 33587200 | tf_op jit(solution)/shard_map/while/body/eval_jaxpr/gather | solution.py:26
  2963.7 48.7 %gather_fusion = bf16[8192,1024]{1,0:T(8,128)(2,1)} fusion(bf16[8192,1024]{1,0:T(8,128)(2,1)} %get-tuple-element.254, s32[8192]{0:T(1024)S(1)} %get-tuple-element.211), kind=kCustom, calls=%fused_computation.clone.1 | custom fusion | bytes 33587200 | tf_op jit(solution)/shard_map/while/body/eval_jaxpr/gather | solution.py:25
  3031.9 21.4 bitcast_multiply_fusion.4
  3053.3 92.5 %scatter_fusion = f32[8192,1024]{1,0:T(8,128)} fusion(f32[8192,1024]{1,0:T(8,128)} %get-tuple-element.236, s32[8192]{0:T(1024)S(1)} %bitcast.137, f32[8192,1024]{1,0:T(8,128)} %get-tuple-element.217), kind=kCustom, calls=%fused_computation.4.clone.1 | custom fusion | flops 8388608 | bytes 100696064 | tf_op jit(solution)/shard_map/while/body/eval_jaxpr/scatter-add | solution.py:37
  3145.8 92.5 %scatter_fusion.1 = f32[8192,1024]{1,0:T(8,128)} fusion(f32[8192,1024]{1,0:T(8,128)} %get-tuple-element.237, s32[8192]{0:T(1024)S(1)} %bitcast.138, f32[8192,1024]{1,0:T(8,128)} %get-tuple-element.218), kind=kCustom, calls=%fused_computation.5.clone.1 | custom fusion | flops 8388608 | bytes 100696064 | tf_op jit(solution)/shard_map/while/body/eval_jaxpr/scatter-add | solution.py:38
  3238.3 17.5 convert_element_type.54
  3255.8 19.9 all-to-all-start.3
  3275.8 17.5 convert_element_type.58
  3293.3 212.4 %all-to-all-done.3 = bf16[128,64,1024]{2,1,0:T(8,128)(2,1)} async-done(((bf16[128,64,1024]{2,1,0:T(8,128)(2,1)}), bf16[128,64,1024]{2,1,0:T(8,128)(2,1)}, u32[]{:S(2)}, u32[]{:S(2)}) %all-to-all-start.3) | async-done | bytes 16777248 | tf_op jit(solution)/shard_map/all_to_all | solution.py:61
  3505.7 19.9 all-to-all-start.4
  3527.1 68.6 %scatter_custom_fusion.2 = f32[128,1024]{1,0:T(8,128)S(1)} fusion(s32[8192]{0:T(1024)S(1)} %reshape.220, bf16[8192,1024]{1,0:T(8,128)(2,1)} %bitcast.41, f32[]{:T(128)} %constant.9.clone.1), kind=kCustom, calls=%fused_computation.48 | custom fusion | flops 16777216 | bytes 17301508 | tf_op jit(solution)/shard_map/scatter-add | solution.py:64
  3596.5 159.1 %all-to-all-done.4 = bf16[128,64,1024]{2,1,0:T(8,128)(2,1)} async-done(((bf16[128,64,1024]{2,1,0:T(8,128)(2,1)}), bf16[128,64,1024]{2,1,0:T(8,128)(2,1)}, u32[]{:S(2)}, u32[]{:S(2)}) %all-to-all-start.4) | async-done | bytes 16777248 | tf_op jit(solution)/shard_map/all_to_all | solution.py:62
  3755.6 68.6 %scatter_custom_fusion.3 = f32[128,1024]{1,0:T(8,128)S(1)} fusion(s32[8192]{0:T(1024)S(1)} %reshape.220, bf16[8192,1024]{1,0:T(8,128)(2,1)} %bitcast.42, f32[]{:T(128)} %constant.9.clone.1), kind=kCustom, calls=%fused_computation.46 | custom fusion | flops 16777216 | bytes 17301508 | tf_op jit(solution)/shard_map/scatter-add | solution.py:65
  (207 shorter events, 197.9 us)
Async XLA Ops:
  0.6 19.9 copy-start
  19.8 0.6 copy-start.5
  56.0 7.6 copy-start.2
  56.0 237.6 %all-to-all-start.2 = ((bf16[128,64,1024]{2,1,0:T(8,128)(2,1)}), bf16[128,64,1024]{2,1,0:T(8,128)(2,1)}, u32[]{:S(2)}, u32[]{:S(2)}) async-start(bf16[128,64,1024]{2,1,0:T(8,128)(2,1)} %bitcast.136), calls=%async_computation.2 | async-start | bytes 33554432 | tf_op jit(solution)/shard_map/all_to_all | solution.py:59
  293.6 20.0 copy-start.7
  293.6 21.0 copy-start.8
  293.6 249.9 %all-to-all-start.1 = ((bf16[128,64,1024]{2,1,0:T(8,128)(2,1)}), bf16[128,64,1024]{2,1,0:T(8,128)(2,1)}, u32[]{:S(2)}, u32[]{:S(2)}) async-start(bf16[128,64,1024]{2,1,0:T(8,128)(2,1)} %bitcast.134), calls=%async_computation.1 | async-start | bytes 33554432 | tf_op jit(solution)/shard_map/all_to_all | solution.py:58
  566.1 116.2 %copy-start.3 = (f32[8,64,128]{2,1,0:T(8,128)}, f32[8,64,128]{2,1,0:T(8,128)S(1)}, u32[]{:S(2)}) copy-start(f32[8,64,128]{2,1,0:T(8,128)S(1)} %get-tuple-element.253) | copy-start | bytes 786436 | tf_op jit(solution)/shard_map/while
  674.1 16.5 slice-start
  674.1 16.5 slice-start.1
  674.1 16.5 slice-start.2
  682.3 8.3 slice-start.3
  807.6 92.5 %copy-start.4 = (f32[8,64,128]{2,1,0:T(8,128)S(1)}, f32[8,64,128]{2,1,0:T(8,128)}, u32[]{:S(2)}) copy-start(f32[8,64,128]{2,1,0:T(8,128)} %copy-done.3) | copy-start | bytes 786436 | tf_op jit(solution)/shard_map/while
  900.1 116.2 %copy-start.3 = (f32[8,64,128]{2,1,0:T(8,128)}, f32[8,64,128]{2,1,0:T(8,128)S(1)}, u32[]{:S(2)}) copy-start(f32[8,64,128]{2,1,0:T(8,128)S(1)} %get-tuple-element.253) | copy-start | bytes 786436 | tf_op jit(solution)/shard_map/while
  1008.1 16.5 slice-start
  1008.1 16.5 slice-start.1
  1008.1 16.5 slice-start.2
  1016.4 8.3 slice-start.3
  1141.6 92.5 %copy-start.4 = (f32[8,64,128]{2,1,0:T(8,128)S(1)}, f32[8,64,128]{2,1,0:T(8,128)}, u32[]{:S(2)}) copy-start(f32[8,64,128]{2,1,0:T(8,128)} %copy-done.3) | copy-start | bytes 786436 | tf_op jit(solution)/shard_map/while
  1234.2 116.2 %copy-start.3 = (f32[8,64,128]{2,1,0:T(8,128)}, f32[8,64,128]{2,1,0:T(8,128)S(1)}, u32[]{:S(2)}) copy-start(f32[8,64,128]{2,1,0:T(8,128)S(1)} %get-tuple-element.253) | copy-start | bytes 786436 | tf_op jit(solution)/shard_map/while
  1342.2 16.5 slice-start
  1342.2 16.5 slice-start.1
  1342.2 16.5 slice-start.2
  1350.4 8.3 slice-start.3
  1475.6 92.5 %copy-start.4 = (f32[8,64,128]{2,1,0:T(8,128)S(1)}, f32[8,64,128]{2,1,0:T(8,128)}, u32[]{:S(2)}) copy-start(f32[8,64,128]{2,1,0:T(8,128)} %copy-done.3) | copy-start | bytes 786436 | tf_op jit(solution)/shard_map/while
  1568.2 116.2 %copy-start.3 = (f32[8,64,128]{2,1,0:T(8,128)}, f32[8,64,128]{2,1,0:T(8,128)S(1)}, u32[]{:S(2)}) copy-start(f32[8,64,128]{2,1,0:T(8,128)S(1)} %get-tuple-element.253) | copy-start | bytes 786436 | tf_op jit(solution)/shard_map/while
  1676.2 16.5 slice-start
  1676.2 16.5 slice-start.1
  1676.2 16.5 slice-start.2
  1684.4 8.3 slice-start.3
  1809.7 92.5 %copy-start.4 = (f32[8,64,128]{2,1,0:T(8,128)S(1)}, f32[8,64,128]{2,1,0:T(8,128)}, u32[]{:S(2)}) copy-start(f32[8,64,128]{2,1,0:T(8,128)} %copy-done.3) | copy-start | bytes 786436 | tf_op jit(solution)/shard_map/while
  1902.2 116.2 %copy-start.3 = (f32[8,64,128]{2,1,0:T(8,128)}, f32[8,64,128]{2,1,0:T(8,128)S(1)}, u32[]{:S(2)}) copy-start(f32[8,64,128]{2,1,0:T(8,128)S(1)} %get-tuple-element.253) | copy-start | bytes 786436 | tf_op jit(solution)/shard_map/while
  2010.2 16.5 slice-start
  2010.2 16.5 slice-start.1
  2010.2 16.5 slice-start.2
  2018.5 8.3 slice-start.3
  2143.7 92.5 %copy-start.4 = (f32[8,64,128]{2,1,0:T(8,128)S(1)}, f32[8,64,128]{2,1,0:T(8,128)}, u32[]{:S(2)}) copy-start(f32[8,64,128]{2,1,0:T(8,128)} %copy-done.3) | copy-start | bytes 786436 | tf_op jit(solution)/shard_map/while
  2236.2 116.2 %copy-start.3 = (f32[8,64,128]{2,1,0:T(8,128)}, f32[8,64,128]{2,1,0:T(8,128)S(1)}, u32[]{:S(2)}) copy-start(f32[8,64,128]{2,1,0:T(8,128)S(1)} %get-tuple-element.253) | copy-start | bytes 786436 | tf_op jit(solution)/shard_map/while
  2344.3 16.5 slice-start
  2344.3 16.5 slice-start.1
  2344.3 16.5 slice-start.2
  2352.5 8.3 slice-start.3
  2477.7 92.5 %copy-start.4 = (f32[8,64,128]{2,1,0:T(8,128)S(1)}, f32[8,64,128]{2,1,0:T(8,128)}, u32[]{:S(2)}) copy-start(f32[8,64,128]{2,1,0:T(8,128)} %copy-done.3) | copy-start | bytes 786436 | tf_op jit(solution)/shard_map/while
  2570.3 116.2 %copy-start.3 = (f32[8,64,128]{2,1,0:T(8,128)}, f32[8,64,128]{2,1,0:T(8,128)S(1)}, u32[]{:S(2)}) copy-start(f32[8,64,128]{2,1,0:T(8,128)S(1)} %get-tuple-element.253) | copy-start | bytes 786436 | tf_op jit(solution)/shard_map/while
  2678.3 16.5 slice-start
  2678.3 16.5 slice-start.1
  2678.3 16.5 slice-start.2
  2686.5 8.3 slice-start.3
  2811.8 92.5 %copy-start.4 = (f32[8,64,128]{2,1,0:T(8,128)S(1)}, f32[8,64,128]{2,1,0:T(8,128)}, u32[]{:S(2)}) copy-start(f32[8,64,128]{2,1,0:T(8,128)} %copy-done.3) | copy-start | bytes 786436 | tf_op jit(solution)/shard_map/while
  2904.3 116.2 %copy-start.3 = (f32[8,64,128]{2,1,0:T(8,128)}, f32[8,64,128]{2,1,0:T(8,128)S(1)}, u32[]{:S(2)}) copy-start(f32[8,64,128]{2,1,0:T(8,128)S(1)} %get-tuple-element.253) | copy-start | bytes 786436 | tf_op jit(solution)/shard_map/while
  3012.3 16.5 slice-start
  3012.3 16.5 slice-start.1
  3012.3 16.5 slice-start.2
  3020.6 8.3 slice-start.3
  3145.8 92.5 %copy-start.4 = (f32[8,64,128]{2,1,0:T(8,128)S(1)}, f32[8,64,128]{2,1,0:T(8,128)}, u32[]{:S(2)}) copy-start(f32[8,64,128]{2,1,0:T(8,128)} %copy-done.3) | copy-start | bytes 786436 | tf_op jit(solution)/shard_map/while
  3255.8 249.9 %all-to-all-start.3 = ((bf16[128,64,1024]{2,1,0:T(8,128)(2,1)}), bf16[128,64,1024]{2,1,0:T(8,128)(2,1)}, u32[]{:S(2)}, u32[]{:S(2)}) async-start(bf16[128,64,1024]{2,1,0:T(8,128)(2,1)} %bitcast.135), calls=%async_computation.3 | async-start | bytes 33554432 | tf_op jit(solution)/shard_map/all_to_all | solution.py:61
  3505.7 20.5 copy-start.6
  3505.7 249.9 %all-to-all-start.4 = ((bf16[128,64,1024]{2,1,0:T(8,128)(2,1)}), bf16[128,64,1024]{2,1,0:T(8,128)(2,1)}, u32[]{:S(2)}, u32[]{:S(2)}) async-start(bf16[128,64,1024]{2,1,0:T(8,128)(2,1)} %bitcast.133), calls=%async_computation.4 | async-start | bytes 33554432 | tf_op jit(solution)/shard_map/all_to_all | solution.py:62
  3527.1 297.9 %copy-start.1 = (bf16[128,1024]{1,0:T(8,128)(2,1)S(1)}, bf16[128,1024]{1,0:T(8,128)(2,1)}, u32[]{:S(2)}) copy-start(bf16[128,1024]{1,0:T(8,128)(2,1)} %param.15) | copy-start | bytes 786436
where the time goes:
time: 3840 us; the launch traced here: 3820 us
  other arithmetic  1850 us (48%)
  local copies, waits for them, and re-layouts  882 us (23%)
  waiting for transfers between devices  794 us (21%)
  matrix products  214 us (6%)
  starting transfers between devices  67.4 us (2%)
    scatter-add x8, other arithmetic, scan_step(): acc_down = acc_down.at[flat_slots].add(down_part.reshape(-1, width))  740 us
    scatter-add x8, other arithmetic, scan_step(): acc_up = acc_up.at[flat_slots].add(up_part.reshape(-1, width))  740 us
    gather x8, local copies, waits for them, and re-layouts, scan_step(): up_rows = up_table[slot_blk]  389 us
    gather x8, local copies, waits for them, and re-layouts, scan_step(): down_rows = down_table[slot_blk]  389 us
    all_to_all x1, waiting for transfers between devices, per_device(): lax.all_to_all(up_local[asked_rows], 'ep', 0, 0, tiled=True)  228 us
    all_to_all x1, waiting for transfers between devices, per_device(): lax.all_to_all(acc_up.astype(jnp.bfloat16).reshape(n_group, n_req, width)...  212 us
    all_to_all x1, waiting for transfers between devices, per_device(): lax.all_to_all(down_local[asked_rows], 'ep', 0, 0, tiled=True)  194 us
    mul x16, other arithmetic, scan_step(): down_part = w_out.astype(jnp.float32)[:, :, None] * dy_blk[:, None, :]  171 us
  transfers between devices with their start and end apart: 4, of which 4 were waited for; matrix products, arithmetic and copies ran while one was open for 3% of the time, Pallas kernels for 0%

commit v1 on v0

v1 whole, which is shorter than its diff:
```python
import functools
import math
import jax
import jax.numpy as jnp
from jax import lax
from jax.experimental import pallas as pl
from jax.experimental.pallas import tpu as pltpu
from jax.sharding import PartitionSpec as P


CORE, ZTOK, ZTAB = 1, 32, 96
N_EP = ROWS = LANES = 128
REQ, SUB, TILE, RING = 64, 16, 8, 4
OWN, NEXT, OPP, PREV = range(RING)
HERE, THERE = UP, DOWN = PAIR = range(2)
N_SET, N_OWN = 4, 32
SETS = range(N_SET)
SET_ME, SET_CORE, SET_FAR, SET_FAR_CORE = SETS
CHIPS = N_OWN // 2
N_GRP = CHIPS // 2
N_HI = N_OWN * REQ // LANES
WIDE = 2 * LANES
G_ROWS = 2 * WIDE
MIB = 2 ** 20
ALL_VMEM = 60 * MIB
F32, BF16 = jnp.float32, jnp.bfloat16
NN, NT = ((((1,), (side,)), ((), ())) for side in PAIR)


def span(i, size):
    return slice(i * size, (i + 1) * size)


def aligned(start, size):
    return pl.ds(pl.multiple_of(start, size), size)


def steps(count, body):
    lax.fori_loop(0, count, lambda i, carry: (body(i), carry)[1], 0)


def start_all(copies):
    for copy in copies:
        copy.start()


def wait_all(copies):
    for copy in copies:
        copy.wait()


def gelu_pair(pre_act):
    normal_cdf = 0.5 * (1.0 + lax.erf(pre_act * (2.0 ** -0.5)))
    normal_pdf = jnp.exp(-0.5 * pre_act * pre_act) * ((2.0 * math.pi) ** -0.5)
    return pre_act * normal_cdf, normal_cdf + pre_act * normal_pdf


def dot(a, b, dims=NN):
    return lax.dot_general(a, b, dims, preferred_element_type=F32)


class Side:
    pass


class Place:
    def __init__(self):
        me = lax.axis_index('ep')
        self.core, x, y, z = me % 2, (me // 2) % RING, (me // TILE) % RING, me // N_OWN
        self.z = z

        def device(z_to, y_to, x_to):
            return ((z_to * RING + y_to) * RING + x_to) * 2 + self.core

        self.plane_peer = device(3 - z, y, x)
        self.core_peer = me + 1 - 2 * self.core
        self.far_peer = device(z + 1 - 2 * (z % 2), y, x)
        along_x = [device(z, y, (x + step) % RING) for step in (NEXT, PREV)]
        along_y = [device(z, (y + step) % RING, x) for step in (NEXT, PREV)]
        self.peers = (*along_x, *along_y, self.plane_peer, self.core_peer, self.far_peer)
        self.chip = y * RING + x
        self.sides = []
        for k, (first, second, axes) in enumerate(((x, y, (along_x, along_y)), (y, x, (along_y, along_x)))):
            one = Side()
            one.k, one.first, one.second = k, first, second
            one.axis1, one.axis2 = axes
            self.sides.append(one)

    def meet(self):
        barrier = pltpu.get_barrier_semaphore()
        for peer in self.peers:
            pl.semaphore_signal(barrier, inc=1, device_id={'ep': peer}, device_id_type=pl.DeviceIdType.MESH)
        pl.semaphore_wait(barrier, len(self.peers))


def chip_at(one, shift1, shift2):
    first, second = (one.first + shift1) % RING, (one.second + shift2) % RING
    return first * RING + second if one.k else second * RING + first


def remote(src, dst, sems, index, peer):
    return pltpu.make_async_remote_copy(src_ref=src, dst_ref=dst, send_sem=sems[UP].at[index], recv_sem=sems[DOWN].at[index],
                                        device_id={'ep': peer}, device_id_type=pl.DeviceIdType.MESH)


NEAR1, FAR1, NEAR2, FAR2, N_PIECE = 0, 4, 6, 22, 30
TOK_STEP = 64


def head_kernel(x_ref, dy_ref, meta_ref, u_ref, v_ref,
                u_all, v_far, x1, x2, x3, dy1, dy2, dy3, g0, g1, g2, g3, p_hot, pt_hot,
                u_own, meta_v, gates_v, hi_ref, lo_ref, a1_ref, a2_ref, a3_ref, row_v, p_v, pt_v,
                u_send, u_recv, meta_send, meta_recv, tok_send, tok_recv, tab_send, tab_recv, u_sem, meta_sem, gate_sem, p_sem, pt_sem):
    n_tok, width = x_ref.shape
    rows = u_ref.shape[0]
    half = width // 2
    n_chunk = n_tok // TOK_STEP
    at = Place()
    sides = at.sides

    load_u = pltpu.make_async_copy(u_ref, u_own, u_sem)
    load_meta = pltpu.make_async_copy(meta_ref, meta_v.at[SET_ME], meta_sem)
    start_all((load_u, load_meta))
    at.meet()

    chip_row = at.chip * (2 * rows)
    meta_sems, tok_sems, tab_sems = (meta_send, meta_recv), (tok_send, tok_recv), (tab_send, tab_recv)
    meta_core = remote(meta_ref, meta_v.at[SET_CORE], meta_sems, SET_ME, at.core_peer)
    meta_far = remote(meta_ref, meta_v.at[SET_FAR], meta_sems, SET_CORE, at.far_peer)
    meta_pass = remote(meta_v.at[SET_FAR], meta_v.at[SET_FAR_CORE], meta_sems, SET_FAR, at.core_peer)
    tok_far = [remote(src, dst, tok_sems, (SET_ME, i), at.far_peer) for i, (src, dst) in enumerate(((x_ref, x2), (dy_ref, dy2)))]
    tok_core = [remote(src, dst, tok_sems, (SET_CORE, i), at.core_peer) for i, (src, dst) in enumerate(((x_ref, x1), (dy_ref, dy1)))]
    tok_pass = [remote(src, dst, tok_sems, (SET_FAR, i), at.core_peer) for i, (src, dst) in enumerate(((x2, x3), (dy2, dy3)))]
    swap_u = remote(u_ref, u_all.at[aligned(chip_row + rows, rows)], tab_sems, UP, at.plane_peer)
    swap_v = remote(v_ref, v_far, tab_sems, DOWN, at.plane_peer)

    def piece(one, shift1, shift2, w):
        return u_all.at[aligned(chip_at(one, shift1, shift2) * (2 * rows) + w * rows, rows), pl.ds(one.k * half, half)]

    def copy_of(one, number, src, dst, peer):
        return remote(src, dst, (u_send, u_recv), (one.k, number), peer)

    def send(one, number, shift1, shift2, w, peer):
        place = piece(one, shift1, shift2, w)
        mine = (shift1, shift2, w) == (OWN, OWN, HERE)
        copy_of(one, number, u_own.at[:, pl.ds(one.k * half, half)] if mine else place, place, peer).start()

    def landed(one, number, shift1, shift2, w):
        place = piece(one, shift1, shift2, w)
        copy_of(one, number, place, place, one.axis1[UP]).wait_recv()

    def spread_first(one, w):
        for d in PAIR:
            send(one, NEAR1 + d * 2 + w, OWN, OWN, w, one.axis1[d])

    def spread_second(one, r, w):
        for d in PAIR:
            send(one, NEAR2 + d * TILE + r * 2 + w, r, OWN, w, one.axis2[d])

    def pass_second(one, r, w):
        back = NEXT if w else PREV
        landed(one, NEAR2 + w * TILE + r * 2 + w, r, back, w)
        send(one, FAR2 + r * 2 + w, r, back, w, one.axis2[w])

    def near_pieces(w):
        for one in sides:
            landed(one, NEAR1 + w, PREV, OWN, w)
            if w == HERE:
                send(one, FAR1 + w, PREV, OWN, w, one.axis1[UP])
            spread_second(one, PREV, w)
            landed(one, NEAR1 + 2 + w, NEXT, OWN, w)
            if w == THERE:
                send(one, FAR1 + w, NEXT, OWN, w, one.axis1[DOWN])
            spread_second(one, NEXT, w)

    def partner_plane():
        swap_u.wait_recv()
        for one in sides:
            spread_first(one, THERE)
            spread_second(one, OWN, THERE)

    def opposite_pieces(w):
        for one in sides:
            landed(one, FAR1 + w, OPP, OWN, w)
            spread_second(one, OPP, w)

    def pass_on(w, *which):
        for r in which:
            for one in sides:
                pass_second(one, r, w)

    def meta_arrives():
        meta_far.wait_recv()
        meta_pass.start()

    events = (
        (4, lambda: near_pieces(HERE)),
        (7, partner_plane),
        (8, meta_core.wait_recv),
        (9, lambda: opposite_pieces(HERE)),
        (13, meta_arrives),
        (14, lambda: pass_on(HERE, OWN)),
        (17, lambda: near_pieces(THERE)),
        (20, lambda: pass_on(HERE, PREV, NEXT)),
        (22, lambda: opposite_pieces(THERE)),
        (24, meta_pass.wait_recv),
        (25, lambda: pass_on(HERE, OPP)),
        (27, lambda: pass_on(THERE, OWN)),
        (29, lambda: pass_on(THERE, PREV, NEXT)),
    )

    start_all((meta_far, swap_u, swap_v, meta_core))
    load_u.wait()
    for one in sides:
        spread_first(one, HERE)
        spread_second(one, OWN, HERE)
    store_u = pltpu.make_async_copy(u_own, u_all.at[aligned(chip_row, rows)], u_sem)
    start_all((store_u, *tok_far, *tok_core))
    load_meta.wait()

    packed = (SUB, LANES)
    row_iota = lax.broadcasted_iota(jnp.int32, packed, 0).astype(F32)
    iotas = [(row_iota + float(SUB) * k).astype(BF16) for k in range(SUB)]
    zero, unit = jnp.zeros(packed, BF16), jnp.ones(packed, BF16)

    def set_up(s):
        slot = meta_v[s, :n_tok, :].astype(jnp.int32)
        owner = slot >> 6
        z_of = owner >> 5
        same_plane = z_of == at.z
        here = ((owner & 1) == at.core) & (same_plane | (z_of == 3 - at.z))
        local = ((((owner >> 1) & 15) * 2 + jnp.where(same_plane, HERE, THERE)) << 6) + (slot & 63)
        hi_ref[...] = jnp.where(here, local >> 7, 255).astype(F32)
        lo_ref[...] = (local & 127).astype(F32)
        gate = meta_v[s, span(1, n_tok), :]
        first = gate.astype(BF16).astype(F32)
        second = (gate - first).astype(BF16).astype(F32)
        a1_ref[...] = first
        a2_ref[...] = second
        a3_ref[...] = (gate - first) - second

    def spread(row):
        return jnp.broadcast_to(row, packed).astype(BF16)

    def one_hot(row, count):
        return jnp.concatenate([jnp.where(row == one_iota, unit, zero) for one_iota in iotas[:count]], axis=0)

    def one_token(t):
        row = pl.ds(t, 1)
        hit = spread(hi_ref[row, :]) == iotas[0]
        lhs = jnp.concatenate([jnp.where(hit, spread(ref[row, :]), zero) for ref in (a1_ref, a2_ref, a3_ref)], axis=0)
        return lhs, one_hot(spread(lo_ref[row, :]), TILE)

    def two_tokens(t):
        lhs_a, rhs_a = one_token(t)
        lhs_b, rhs_b = one_token(t + 1)
        empty = jnp.zeros_like(lhs_a)
        lhs = jnp.concatenate([jnp.concatenate(pair, axis=1) for pair in ((lhs_a, empty), (empty, lhs_b))], axis=0)
        res = dot(lhs, jnp.concatenate([rhs_a, rhs_b], axis=1), NT)
        low_a, mid_a, top_a, low_b, mid_b, top_b = (res[span(k, SUB)] for k in range(6))
        return (top_a + mid_a) + low_a, (top_b + mid_b) + low_b

    def gate_step(i):
        for when, event in events:
            pl.when(i == when * n_chunk // TILE)(event)
        s, j = i // n_chunk, i % n_chunk
        pl.when(j == 0)(lambda: set_up(s))
        for k in range(0, TOK_STEP, 2):
            base = (i * (TOK_STEP // TILE) + k // TILE) * (TILE * N_HI) + k % TILE
            for which, row in enumerate(two_tokens(j * TOK_STEP + k)):
                gates_v[pl.ds(base + which, N_HI, stride=TILE), :] = row

    steps(N_SET * n_chunk, gate_step)
    gate_out = [pltpu.make_async_copy(gates_v.at[pl.ds(s * n_tok * N_HI, n_tok * N_HI)], ref, gate_sem.at[s]) for s, ref in enumerate((g0, g1, g2, g3))]
    start_all(gate_out)
    pass_on(THERE, OPP)

    for s in SETS:
        asked = [meta_v[s, pl.ds(2 * n_tok + z_of * CHIPS, CHIPS), :] for z_of in (at.z, 3 - at.z)]
        turned = [jnp.concatenate([one_req[:, REQ:], one_req[:, :REQ]], axis=1) for one_req in asked]
        low_core = at.core == 0
        lane = lax.broadcasted_iota(jnp.int32, (CHIPS, LANES), 1)
        row_v[s] = jnp.where(lane < REQ, jnp.where(low_core, asked[HERE], turned[HERE]), jnp.where(low_core, turned[THERE], asked[THERE]) + float(ROWS))

    def hot_step(chip):
        for s in SETS:
            hot = one_hot(spread(row_v[s, pl.ds(chip, 1), :]), SUB)
            pt_v[chip, s] = hot
            p_v[chip, span(s, LANES), :] = hot.astype(F32).T.astype(BF16)

    steps(CHIPS, hot_step)
    hot_out = [pltpu.make_async_copy(p_v, p_hot, p_sem), pltpu.make_async_copy(pt_v, pt_hot, pt_sem)]
    start_all(hot_out)

    tok_far[UP].wait_recv()
    tok_pass[UP].start()
    for one in sides:
        for r in range(RING):
            landed(one, NEAR2 + TILE + r * 2, r, NEXT, HERE)
            landed(one, NEAR2 + r * 2 + 1, r, PREV, THERE)
    for one in sides:
        for r in range(RING):
            for w in PAIR:
                landed(one, FAR2 + r * 2 + w, r, OPP, w)
    swap_v.wait_recv()
    tok_far[DOWN].wait_recv()
    tok_pass[DOWN].start()
    for copy in tok_core + tok_pass:
        copy.wait_recv()
    wait_all(gate_out + hot_out + [store_u])
    for one in sides:
        for number in range(N_PIECE):
            place = piece(one, OWN, OWN, HERE)
            copy_of(one, number, place, place, one.axis1[UP]).wait_send()
    for copy in tok_far + tok_core + tok_pass + [meta_core, meta_far, meta_pass, swap_u, swap_v]:
        copy.wait_send()


def vmem(dtype, *shapes):
    return [pltpu.VMEM(shape, dtype) for shape in shapes]


def dma_sems(*shapes):
    return [pltpu.SemaphoreType.DMA(shape) for shape in shapes]


def arrays(dtype, *shapes):
    return [jax.ShapeDtypeStruct(shape, dtype) for shape in shapes]


def kernel(body, out_shape, scratch, flops, mib, grid=(), comm=None, **specs):
    extra = {} if comm is None else dict(collective_id=comm, has_side_effects=True)
    return pl.pallas_call(
        body, grid=grid, out_shape=out_shape, scratch_shapes=scratch,
        compiler_params=pltpu.CompilerParams(vmem_limit_bytes=ALL_VMEM, **extra),
        cost_estimate=pl.CostEstimate(flops=flops, bytes_accessed=mib * MIB, transcendentals=0), **specs)


ANY, IN_VMEM = pl.BlockSpec(memory_space=pl.ANY), pl.BlockSpec(memory_space=pltpu.VMEM)


def head_pass(x, dy, meta, u_local, v_local):
    n_tok, width = x.shape
    rows = u_local.shape[0]
    gate, p_shape, pt_shape = (n_tok * N_HI, LANES), (CHIPS, N_SET * LANES, WIDE), (CHIPS, N_SET, WIDE, LANES)
    outs = arrays(BF16, (N_OWN * rows, width), u_local.shape, *[x.shape] * 6) + arrays(F32, *[gate] * N_SET) + arrays(BF16, p_shape, pt_shape)
    pieces, three, six, two = (2, N_PIECE), (3,), (3, 2), (2,)
    scratch = vmem(BF16, u_local.shape) + vmem(F32, (N_SET, *meta.shape), (N_SET * n_tok * N_HI, LANES), *[(n_tok, LANES)] * 5, (N_SET, CHIPS, LANES))
    scratch += vmem(BF16, p_shape, pt_shape) + dma_sems(pieces, pieces, three, three, six, six, two, two, (), (), (N_SET,), (), ())
    u_all, v_far, x1, x2, x3, dy1, dy2, dy3, *gates, p_hot, pt_hot = kernel(
        head_kernel, outs, scratch, N_SET * n_tok * 12 * MIB, 60, comm=1,
        in_specs=[ANY] * 5, out_specs=[ANY] * len(outs))(x, dy, meta, u_local, v_local)
    gates = [one.reshape(n_tok // TILE, N_HI, TILE, LANES) for one in gates]
    return u_all, v_far, (x, x1, x2, x3), (dy, dy1, dy2, dy3), gates, p_hot.reshape(N_GRP, 2, *p_shape[1:]), pt_hot.reshape(N_GRP, 2, *pt_shape[1:])


def block(shape, axis=0):
    return pl.BlockSpec(shape, lambda g: tuple(g if k == axis else 0 for k in range(len(shape))))


def whole(arr):
    return pl.BlockSpec(arr.shape, lambda g: (0,) * arr.ndim, pipeline_mode=pl.Buffered(1))


P_BLOCK, PT_BLOCK = block((1, 2, N_SET * LANES, WIDE)), block((1, 2, N_SET, WIDE, LANES))


def pick_rows(p_ref, tables, out_ref):
    for i in PAIR:
        rows = dot(p_ref[0, i], tables[i]).astype(BF16)
        for s in SETS:
            out_ref[0, s, span(i, LANES), :] = rows[span(s, LANES)]


def halves(n_tok):
    half = max(n_tok // 2, SUB)
    return [slice(t, t + half) for t in range(0, n_tok, half)]


def staggered(front, back):
    for s in SETS:
        front(s)
        if s:
            back(s - 1)
    back(SET_FAR_CORE)


def spread_slots(pt_ref, values_ref, out, s, n_tok):
    for i in PAIR:
        out[span(i, WIDE), span(s, n_tok)] = dot(pt_ref[0, i, s], values_ref[span(s, n_tok), span(i, LANES)], NT).astype(BF16)


def first_kernel(n_tok, u_ref, p_ref, pt_ref, *refs):
    g_refs, x_refs, dy_refs = (refs[span(i, N_SET)] for i in range(3))
    uc_ref, w_ref, s_ref, dv_ref, wrt, pre = refs[3 * N_SET:]
    tok_chunk = min(TOK_STEP, n_tok)

    def front(s):
        for part in halves(n_tok):
            pre[s, part, :] = dot(x_refs[s][part, :], uc_ref[0, s], NT)

    def back(s):
        for t in range(n_tok // tok_chunk):
            rows = span(s * (n_tok // tok_chunk) + t, tok_chunk)
            for i in PAIR:
                gate = g_refs[s][span(t, tok_chunk // TILE), i].reshape(tok_chunk, LANES)
                act, slope = gelu_pair(pre[s, span(t, tok_chunk), span(i, LANES)])
                used = gate > 0.0
                w_ref[rows, span(i, LANES)] = jnp.where(used, gate * act, 0.0).astype(BF16)
                s_ref[rows, span(i, LANES)] = jnp.where(used, gate * slope, 0.0)
        spread_slots(pt_ref, w_ref, wrt, s, n_tok)

    pick_rows(p_ref, [u_ref[span(i, WIDE), :] for i in PAIR], uc_ref)
    staggered(front, back)
    dy_all = jnp.concatenate([ref[...] for ref in dy_refs], axis=0)
    dv_ref[...] = dot(wrt[...], dy_all).astype(BF16)


def first_pass(u_all, p_hot, pt_hot, gates, xs, dys):
    n_tok, width = xs[0].shape
    all_tok, slots = N_SET * n_tok, N_GRP * WIDE
    flops = 2 * N_GRP * (N_SET * WIDE * WIDE * width + all_tok * (width * WIDE + LANES * G_ROWS + G_ROWS * width))
    return kernel(
        functools.partial(first_kernel, n_tok),
        arrays(BF16, (N_GRP, N_SET, WIDE, width), (all_tok, slots)) + arrays(F32, (all_tok, slots)) + arrays(BF16, u_all.shape),
        vmem(BF16, (G_ROWS, all_tok)) + vmem(F32, (N_SET, n_tok, WIDE)), flops, 76, grid=(N_GRP,),
        in_specs=[block((G_ROWS, width)), P_BLOCK, PT_BLOCK] + [block((n_tok // TILE, 2, TILE, LANES), axis=1)] * N_SET + [whole(one) for one in (*xs, *dys)],
        out_specs=[block((1, N_SET, WIDE, width)), block((all_tok, WIDE), axis=1), block((all_tok, WIDE), axis=1), block((G_ROWS, width))],
    )(u_all, p_hot, pt_hot, *gates, *xs, *dys)


def down_kernel(n_tok, v_ref, vf_ref, p_ref, w_ref, vc_ref, *y_refs):
    @pl.when(pl.program_id(0) == 0)
    def _():
        for y_ref in y_refs:
            y_ref[...] = jnp.zeros_like(y_ref)

    pick_rows(p_ref, [jnp.concatenate([ref[span(i, ROWS), :] for ref in (v_ref, vf_ref)], axis=0) for i in PAIR], vc_ref)
    for s in SETS:
        y_refs[s][...] += dot(w_ref[span(s, n_tok), :], vc_ref[0, s])


def down_pass(v_own, v_far, p_hot, w_all):
    width = v_own.shape[1]
    all_tok = w_all.shape[0]
    n_tok = all_tok // N_SET
    flops = 2 * N_GRP * WIDE * width * (N_SET * WIDE + all_tok)
    return kernel(
        functools.partial(down_kernel, n_tok),
        arrays(BF16, (N_GRP, N_SET, WIDE, width)) + arrays(F32, *[(n_tok, width)] * N_SET), [], flops, 44, grid=(N_GRP,),
        in_specs=[block((2 * ROWS, width))] * 2 + [P_BLOCK, block((all_tok, WIDE), axis=1)],
        out_specs=[block((1, N_SET, WIDE, width))] + [block((n_tok, width), axis=None)] * N_SET,
    )(v_own, v_far, p_hot, w_all)


def second_kernel(n_tok, vc_ref, pt_ref, s_ref, *refs):
    x_refs, dy_refs = (refs[span(i, N_SET)] for i in PAIR)
    c_ref, du_ref, crt = refs[2 * N_SET:]

    def front(s):
        for part in halves(n_tok):
            rows = slice(s * n_tok + part.start, s * n_tok + part.stop)
            back_dot = dot(dy_refs[s][part, :], vc_ref[0, s], NT)
            slope = s_ref[rows, :]
            c_ref[rows, :] = jnp.where(slope == 0.0, 0.0, slope * back_dot).astype(BF16)

    staggered(front, lambda s: spread_slots(pt_ref, c_ref, crt, s, n_tok))
    x_all = jnp.concatenate([ref[...] for ref in x_refs], axis=0)
    du_ref[...] = dot(crt[...], x_all).astype(BF16)


def second_pass(vc, pt_hot, slopes, xs, dys):
    n_tok, width = xs[0].shape
    all_tok = N_SET * n_tok
    flops = 2 * N_GRP * all_tok * (width * WIDE + LANES * G_ROWS + G_ROWS * width)
    return kernel(
        functools.partial(second_kernel, n_tok),
        arrays(BF16, slopes.shape, (N_GRP * G_ROWS, width)), vmem(BF16, (G_ROWS, all_tok)), flops, 58, grid=(N_GRP,),
        in_specs=[block((1, N_SET, WIDE, width)), PT_BLOCK, block((all_tok, WIDE), axis=1)] + [whole(one) for one in (*xs, *dys)],
        out_specs=[block((all_tok, WIDE), axis=1), block((G_ROWS, width))],
    )(vc, pt_hot, slopes, *xs, *dys)


HALVES = (OPP, NEXT), (PREV, OWN)
FAR_STEP, PLAIN, SUMMED, FAR_2, PLAIN_2, SUMMED_2, PLANE, N_MSG = 0, 4, 8, 12, 14, 16, 18, 19
N_TILE, CHUNK = 4, 32


def tail_kernel(part_ref, c_ref, uc_ref, out_ref, dx_ref,
                own_step, own_mid, s1, s2, sums, mid, t1, t2, tsum, keep, z_send, z_recv,
                c_buf, uc_buf, dx_part, core_recv, far_send, far_recv,
                send_sem, recv_sem, own_sem, load_sem, core_send_sem, core_recv_sem, far_send_sem, far_recv_sem):
    rows, width = out_ref.shape
    half = width // 2
    chip_rows = 2 * rows
    n_tok = dx_ref.shape[0]
    tile = n_tok // N_TILE
    at = Place()
    sides = at.sides

    def load_set(s):
        slot = s % 2
        return (pltpu.make_async_copy(c_ref.at[pl.ds(s * n_tok, n_tok)], c_buf.at[slot], load_sem.at[s, UP]),
                pltpu.make_async_copy(uc_ref.at[:, s], uc_buf.at[slot], load_sem.at[s, DOWN]))

    loads = [load_set(s) for s in SETS]
    for s in (SET_FAR_CORE, SET_FAR):
        start_all(loads[s])
    at.meet()

    def add_up(n_rows, store, *parts):
        def step(i):
            total = None
            for one_part in parts:
                term = one_part(i)
                total = term if total is None else total + term
            store(aligned(i * CHUNK, CHUNK), total)

        steps(n_rows // CHUNK, step)

    def from_buf(buf, *index, skip=0):
        return lambda i: buf[(*index, aligned(skip + i * CHUNK, CHUNK), slice(None))].astype(F32)

    def into_buf(buf, *index):
        def store(place, total):
            buf[(*index, place, slice(None))] = total.astype(buf.dtype)

        return store

    def own(one, shift1, shift2):
        return part_ref.at[aligned(chip_at(one, shift1, shift2) * chip_rows, chip_rows), pl.ds(one.k * half, half)]

    def message(one, number, src, dst, peer):
        return remote(src, dst, (send_sem, recv_sem), (one.k, number), peer)

    plane_rows = (pl.ds(0, rows), pl.ds(rows, rows))
    STEP = NEXT, PREV
    for one in sides:
        k = one.k
        one.far1 = [[message(one, FAR_STEP + d * 2 + i, own(one, OPP, r), s1.at[k, d, i], one.axis1[d]) for i, r in enumerate(HALVES[d])] for d in PAIR]
        one.plain1 = [[message(one, PLAIN + d * 2 + i, own(one, STEP[d], r), s2.at[k, d, r], one.axis1[d]) for i, r in enumerate(HALVES[1 - d])] for d in PAIR]
        one.summed1 = [[message(one, SUMMED + d * 2 + i, sums.at[k, d, i], s2.at[k, d, r], one.axis1[d]) for i, r in enumerate(HALVES[d])] for d in PAIR]
        one.far2 = [message(one, FAR_2 + d, mid.at[k, OPP, plane_rows[d]], t1.at[k, d], one.axis2[d]) for d in PAIR]
        one.plain2 = [message(one, PLAIN_2 + d, mid.at[k, STEP[d], plane_rows[1 - d]], t2.at[k, d, 1 - d], one.axis2[d]) for d in PAIR]
        one.summed2 = [message(one, SUMMED_2 + d, tsum.at[k, d], t2.at[k, d, d], one.axis2[d]) for d in PAIR]
        one.plane = message(one, PLANE, z_send.at[k], z_recv.at[k], at.plane_peer)
        one.stage = [pltpu.make_async_copy(own(one, STEP[d], r), own_step.at[k, d, i], own_sem.at[k, d * 2 + i]) for d in PAIR for i, r in enumerate(HALVES[d])]
        one.stage += [pltpu.make_async_copy(own(one, OWN, r), own_mid.at[k, r], own_sem.at[k, RING + r]) for r in range(RING)]

    def tile_at(t):
        return aligned(t * tile, tile)

    def core_msg(which, t):
        return remote(dx_part.at[SET_CORE if which else SET_FAR_CORE, tile_at(t)], core_recv.at[which, tile_at(t)],
                      (core_send_sem, core_recv_sem), (which, t), at.core_peer)

    def far_msg(t):
        return remote(far_send.at[tile_at(t)], far_recv.at[tile_at(t)], (far_send_sem, far_recv_sem), t, at.far_peer)

    def dx_tile(s, t):
        dx_part[s, tile_at(t), :] = dot(c_buf[s % 2, tile_at(t), :], uc_buf[s % 2].reshape(N_GRP * WIDE, width))

    def dx_pair(which, sets):
        for s in sets:
            wait_all(loads[s])

        def step(t):
            dx_tile(sets[UP], t)
            core_msg(which, t).start()
            dx_tile(sets[DOWN], t)

        steps(N_TILE, step)

    def row_steps(t, body):
        steps(tile // CHUNK, lambda i: body(aligned(t * tile + i * CHUNK, CHUNK)))

    for kind in ('far1', 'plain1'):
        for i in PAIR:
            for one in sides:
                for d in PAIR:
                    getattr(one, kind)[d][i].start()
    for one in sides:
        start_all(one.stage)

    dx_pair(UP, (SET_FAR_CORE, SET_FAR))
    for s in (SET_CORE, SET_ME):
        start_all(loads[s])

    def far_sum(t):
        core_msg(UP, t).wait_recv()

        def add(place):
            far_send[place, :] = dx_part[SET_FAR, place, :] + core_recv[UP, place, :]

        row_steps(t, add)
        far_msg(t).start()

    steps(N_TILE, far_sum)

    for one in sides:
        wait_all(one.stage)
    for i in PAIR:
        for one in sides:
            for d in PAIR:
                one.far1[d][i].wait_recv()
                add_up(chip_rows, into_buf(sums, one.k, d, i), from_buf(own_step, one.k, d, i), from_buf(s1, one.k, d, i))
                one.summed1[d][i].start()

    dx_pair(DOWN, (SET_CORE, SET_ME))

    for i in PAIR:
        for half_way in PAIR:
            r = HALVES[half_way][i]
            for one in sides:
                k = one.k
                one.plain1[1 - half_way][i].wait_recv()
                one.summed1[half_way][i].wait_recv()
                add_up(chip_rows, into_buf(mid, k, r), from_buf(own_mid, k, r), from_buf(s2, k, UP, r), from_buf(s2, k, DOWN, r))
                if r == OPP:
                    start_all(one.far2)
                elif r != OWN:
                    one.plain2[STEP.index(r)].start()
    for one in sides:
        k = one.k
        for d in PAIR:
            one.far2[d].wait_recv()
            add_up(rows, into_buf(tsum, k, d), from_buf(mid, k, STEP[d], skip=d * rows), from_buf(t1, k, d))
            one.summed2[d].start()
    for one in sides:
        k = one.k
        for msg in one.plain2 + one.summed2:
            msg.wait_recv()
        add_up(rows, into_buf(z_send, k), from_buf(mid, k, OWN, skip=rows), from_buf(t2, k, UP, THERE), from_buf(t2, k, DOWN, THERE))
        one.plane.start()
        add_up(rows, into_buf(keep, k), from_buf(mid, k, OWN), from_buf(t2, k, UP, HERE), from_buf(t2, k, DOWN, HERE))
    for one in sides:
        k = one.k
        one.plane.wait_recv()

        def store_out(place, total, k=k):
            out_ref[place, span(k, half)] = total.astype(BF16)

        add_up(rows, store_out, from_buf(keep, k), from_buf(z_recv, k))

    def last_tile(t):
        core_msg(DOWN, t).wait_recv()
        far_msg(t).wait_recv()

        def add(place):
            dx_ref[place, :] = (dx_part[SET_ME, place, :] + core_recv[DOWN, place, :] + far_recv[place, :]).astype(BF16)

        row_steps(t, add)

    steps(N_TILE, last_tile)

    def sent(t):
        for which in PAIR:
            core_msg(which, t).wait_send()
        far_msg(t).wait_send()

    steps(N_TILE, sent)
    for one in sides:
        for pairs in (one.far1, one.plain1, one.summed1):
            for msg in pairs[UP] + pairs[DOWN]:
                msg.wait_send()
        for msg in one.far2 + one.plain2 + one.summed2 + [one.plane]:
            msg.wait_send()


def tail_pass(part, c_all, uc):
    width = part.shape[1]
    rows = part.shape[0] // N_OWN
    n_tok = c_all.shape[0] // N_SET
    half = width // 2
    big, small, toks = (2 * rows, half), (rows, half), (n_tok, width)
    scratch = vmem(BF16, (2, 2, 2, *big), (2, RING, *big), (2, 2, 2, *big), (2, 2, RING, *big), (2, 2, 2, *big), (2, RING, *big), (2, 2, *small), (2, 2, 2, *small), (2, 2, *small))
    scratch += vmem(F32, (2, *small)) + vmem(BF16, (2, *small), (2, *small), (2, n_tok, N_GRP * WIDE), (2, N_GRP, WIDE, width))
    scratch += vmem(F32, (N_SET, *toks), (2, *toks), toks, toks)
    messages, tiles = (2, N_MSG), (2, N_TILE)
    scratch += dma_sems(messages, messages, (2, 2 * RING), (N_SET, 2), tiles, tiles, (N_TILE,), (N_TILE,))
    return kernel(
        tail_kernel, arrays(BF16, (rows, width), toks), scratch, 2 * c_all.size * width, 40, comm=0,
        in_specs=[ANY] * 3, out_specs=[IN_VMEM] * 2)(part, c_all, uc)


def solution(mesh):
    tok_spec, table_spec = P(('dp', 'ep')), P('ep')
    plane = [[z * N_OWN + yx * 2 + c for yx in range(CHIPS)] for z in range(RING) for c in PAIR]

    def swap(arr, mask):
        return lax.ppermute(arr, 'ep', [(i, i ^ mask) for i in range(N_EP)])

    def plane_rows(local):
        return lax.all_gather(local, 'ep', axis=0, tiled=True, axis_index_groups=plane)

    def device_part(tokens, slot_ids, request_rows, gate_vals, grad_out, up_local, down_local):
        n_tok = tokens.shape[0]
        meta = jnp.concatenate([slot_ids.reshape(n_tok, LANES).astype(F32), gate_vals.reshape(n_tok, LANES), request_rows.reshape(REQ, N_EP).astype(F32)])
        v_own = plane_rows(down_local)
        u_all, v_peer, xs, dys, gates, p_hot, pt_hot = head_pass(tokens, grad_out, meta, up_local, down_local)
        v_far = plane_rows(v_peer)
        uc, w_all, slopes, dv_part = first_pass(u_all, p_hot, pt_hot, gates, xs, dys)
        vc, y_own, y_core, y_far, y_far_core = down_pass(v_own, v_far, p_hot, w_all)
        y_for_far, vc = lax.optimization_barrier((y_far + swap(y_far_core, CORE), vc))
        y_from_far = swap(y_for_far, ZTOK)
        y_from_core = swap(y_core, CORE)
        c_all, du_part = second_pass(vc, pt_hot, slopes, xs, dys)
        grad_up, dx = tail_pass(du_part, c_all, uc)
        dv_mine = lax.psum_scatter(dv_part, 'ep', scatter_dimension=0, tiled=True, axis_index_groups=plane)
        dv_mine, y_own, _ = lax.optimization_barrier((dv_mine, y_own, grad_up))
        dv_far = swap(dv_mine[ROWS:], ZTAB)
        y = (y_own + y_from_core + y_from_far).astype(BF16)
        grad_down = (dv_mine[:ROWS].astype(F32) + dv_far.astype(F32)).astype(BF16)
        return y, dx, grad_up, grad_down

    return jax.shard_map(device_part, mesh=mesh, in_specs=(tok_spec,) * 5 + (table_spec,) * 2, out_specs=(tok_spec,) * 4, check_vma=False)
```

time: 3840 us -> 295 us (0.08)
  the two profiles are of different devices: /device:TPU:11 before, /device:TPU:4 now
where the time goes in v1:
time: 295 us; the launch traced here: 294 us
  Pallas kernels  255 us (86%)
  between operations  13.9 us (5%)
  other arithmetic  10.6 us (4%)
  waiting for transfers between devices  8.09 us (3%)
  local copies, waits for them, and re-layouts  4.14 us (1%)
    pallas_call x1, Pallas kernels, head_pass(): kernel(head_kernel, outs, scratch, N_SET * n_tok * 12 * MIB, 60, comm=1,...  77.8 us
    pallas_call x1, Pallas kernels, tail_pass(): kernel(tail_kernel, arrays(BF16, (rows, width), toks), scratch, 2 * c_all...  66.5 us
    pallas_call x1, Pallas kernels, first_pass(): kernel(functools.partial(first_kernel, n_tok), arrays(BF16, (N_GRP, N_SET...  51.1 us
    pallas_call x1, Pallas kernels, second_pass(): kernel(functools.partial(second_kernel, n_tok), arrays(BF16, slopes.shape...  38.6 us
    pallas_call x1, Pallas kernels, down_pass(): kernel(functools.partial(down_kernel, n_tok), arrays(BF16, (N_GRP, N_SET,...  20.7 us
    ppermute x4, waiting for transfers between devices, swap(): return lax.ppermute(arr, 'ep', [(i, i ^ mask) for i in range(N_EP)])  7.32 us
  transfers between devices with their start and end apart: 7, of which 2 were waited for; matrix products, arithmetic and copies ran while one was open for 4% of the time, Pallas kernels for 87%

profile of v1, /device:TPU:4, one launch (start us, length us, event | category | flops | bytes accessed | tf_op | source)
XLA Modules:
  0.0 294.1 jit_solution(1120447538802252846)
XLA Ops:
  7.2 0.0 all-gather.3.cloned.1.call-start
  7.2 0.7 all-gather.3.cloned.1.call-update
  7.9 0.0 all-gather.5.cloned.1.call-start
  7.9 0.8 convert_element_type.26
  8.7 0.1 copy.14
  8.8 0.1 convert_element_type.27
  8.9 1.0 convert_element_type.24
  9.9 0.1 copy.15
  10.0 1.1 copy.16
  11.1 0.8 pad_maximum_fusion.meta_ref
  11.9 77.8 %shard_map.102 = (bf16[4096,1024]{1,0:T(8,128)(2,1)}, bf16[128,1024]{1,0:T(8,128)(2,1)}, bf16[512,1024]{1,0:T(8,128)(2,1)}, bf16[512,1024]{1,0:T(8,128)(2,1)}, b...) custom-call(bf16[512,1024]{1,0:T(8,128)(2,1)} %refs_0_.1, ...), custom_call_target="tpu_custom_call" | custom-call | flops 25769803776 | bytes 62914560 | tf_op jit(solution)/shard_map/pallas_call | solution.py:350
  89.8 0.0 all-gather.5.cloned.1.call-update
  89.8 0.0 reduce-scatter.2.cloned.1.call-start
  89.8 51.1 %shard_map.103 = (bf16[8,4,256,1024]{3,2,1,0:T(8,128)(2,1)}, bf16[2048,2048]{1,0:T(8,128)(2,1)}, f32[2048,2048]{1,0:T(8,128)}, bf16[4096,1024]{1,0:T(8,128)(2,1)}) custom-call(bf16[4096,1024]{1,0:T(8,128)(2,1)} %get-tuple-element.35.u_ref, bf16[8,2,512,256]{3,2,1,0:T(8,128)(2,1)} %bitcast.12, bf16[8,2,4,256,128]{4,3,2,1,0:T(8,128)(2,1)} %bitcast.10, ...), custom_call_target="tpu_custom_call" | custom-call | flops 32212254720 | bytes 79691776 | tf_op jit(solution)/shard_map/pallas_call | solution.py:423
  141.0 0.0 reduce-scatter.2.cloned.1.call-update
  141.0 0.0 all-gather.3.cloned.1.call-done.v_ref
  141.0 0.0 all-gather.5.cloned.1.call-done.vf_ref
  141.1 20.7 %shard_map.104 = (bf16[8,4,256,1024]{3,2,1,0:T(8,128)(2,1)}, f32[512,1024]{1,0:T(8,128)}, f32[512,1024]{1,0:T(8,128)}, f32[512,1024]{1,0:T(8,128)}, f32[512,1024]{1,0:T(8,128)}) custom-call(bf16[2048,1024]{1,0:T(8,128)(2,1)} %all-gather.3.cloned.1.call-done.v_ref, bf16[2048,1024]{1,0:T(8,128)(2,1)} %all-gather.5.cloned.1.call-done.vf_ref, ...), custom_call_target="tpu_custom_call" | custom-call | flops 12884901888 | bytes 46137344 | tf_op jit(solution)/shard_map/pallas_call | solution.py:448
  161.7 0.7 collective-permute-start
  162.5 0.1 collective-permute-start.1
  162.6 3.9 %collective-permute-done = f32[512,1024]{1,0:T(8,128)S(1)} collective-permute-done((f32[512,1024]{1,0:T(8,128)}, f32[512,1024]{1,0:T(8,128)S(1)}, u32[]{:S(2)}, u32[]{:S(2)}) %collective-permute-start) | collective-permute-done | bytes 2097184 | tf_op jit(solution)/shard_map/ppermute | solution.py:691
  166.5 3.5 %add.14 = f32[512,1024]{1,0:T(8,128)} add(f32[512,1024]{1,0:T(8,128)} %get-tuple-element.52, f32[512,1024]{1,0:T(8,128)S(1)} %collective-permute-done) | non-fusion elementwise | flops 524288 | bytes 6291456 | tf_op jit(solution)/shard_map/add | solution.py:704
  170.0 0.0 collective-permute-start.2
  170.0 38.6 %shard_map.105 = (bf16[2048,2048]{1,0:T(8,128)(2,1)}, bf16[4096,1024]{1,0:T(8,128)(2,1)}) custom-call(bf16[8,4,256,1024]{3,2,1,0:T(8,128)(2,1)} %get-tuple-element.55.vc_ref, bf16[8,2,4,256,128]{4,3,2,1,0:T(8,128)(2,1)} %bitcast.11, f32[2048,2048]{1,0:T(8,128)} %get-tuple-element.56.s_ref, bf16[512,1024]{1,0:T(8,128)(2,1)} %refs_0_.1, ...), custom_call_target="tpu_custom_call" | custom-call | flops 27917287424 | bytes 60817408 | tf_op jit(solution)/shard_map/pallas_call | solution.py:476
  208.7 0.0 copy-start
  208.7 66.5 %shard_map.106 = (bf16[128,1024]{1,0:T(8,128)(2,1)}, bf16[512,1024]{1,0:T(8,128)(2,1)}) custom-call(bf16[4096,1024]{1,0:T(8,128)(2,1)} %get-tuple-element.57.part_ref, bf16[2048,2048]{1,0:T(8,128)(2,1)} %get-tuple-element.58.c_ref, bf16[8,4,256,1024]{3,2,1,0:T(8,128)(2,1)} %get-tuple-element.59.uc_ref), custom_call_target="tpu_custom_call" | custom-call | flops 8589934592 | bytes 41943040 | tf_op jit(solution)/shard_map/pallas_call | solution.py:681
  275.2 0.0 reduce-scatter.2.cloned.1.call-done
  275.2 0.0 copy-start.2
  275.2 0.0 copy-start.1
  275.2 1.1 slice.7
  276.3 0.0 copy-start.3
  276.3 1.6 collective-permute-start.3
  278.0 0.0 collective-permute-done.1
  278.0 0.0 collective-permute-done.2
  278.0 0.0 copy-done
  278.0 3.7 %add_convert_fusion = bf16[512,1024]{1,0:T(8,128)(2,1)} fusion(f32[512,1024]{1,0:T(8,128)} %collective-permute-done.2, f32[512,1024]{1,0:T(8,128)S(1)} %copy-done, f32[512,1024]{1,0:T(8,128)} %collective-permute-done.1), kind=kLoop, calls=%fused_computation | loop fusion | flops 1572864 | bytes 7340032 | tf_op jit(solution)/shard_map/convert_element_type | solution.py:712
  281.7 3.4 %collective-permute-done.3 = bf16[128,1024]{1,0:T(8,128)(2,1)S(1)} collective-permute-done((bf16[128,1024]{1,0:T(8,128)(2,1)S(1)}, bf16[128,1024]{1,0:T(8,128)(2,1)S(1)}, u32[]{:S(2)}, u32[]{:S(2)}) %collective-permute-start.3) | collective-permute-done | bytes 262176 | tf_op jit(solution)/shard_map/ppermute | solution.py:691
  285.1 0.0 copy-done.2
  285.1 0.8 add_convert_fusion.1
  285.9 0.0 copy-done.1
  285.9 1.0 copy.19
  286.9 0.0 copy-done.3
  286.9 0.7 copy.20
Async XLA Ops:
  7.2 133.9 %all-gather.3.cloned.1.call-start = ((), (), s32[]{:S(2)}) async-start(), calls=%async_computation.2 | async-start | bytes 4456448 | tf_op jit(solution)/shard_map/all_gather | solution.py:694
  7.9 133.2 %all-gather.5.cloned.1.call-start = ((), (), s32[]{:S(2)}) async-start(), calls=%async_computation.3 | async-start | bytes 4456448 | tf_op jit(solution)/shard_map/all_gather | solution.py:694
  89.8 185.4 %reduce-scatter.2.cloned.1.call-start = ((), (), s32[]{:S(2)}) async-start(), calls=%async_computation.1 | async-start | bytes 8912896 | tf_op jit(solution)/shard_map/reduce_scatter | solution.py:709
  161.7 4.7 %collective-permute-start = (f32[512,1024]{1,0:T(8,128)}, f32[512,1024]{1,0:T(8,128)S(1)}, u32[]{:S(2)}, u32[]{:S(2)}) collective-permute-start(f32[512,1024]{1,0:T(8,128)} %get-tuple-element.53), channel_id=1, source_target_pairs={{0,1},{1,0},{2,3},{3,2},{4,5},{5,4},{6,7},{7,6},{8,9},{9,8},{10,11... | collective-permute-start | bytes 6291464 | tf_op jit(solution)/shard_map/ppermute | solution.py:691
  162.5 115.5 %collective-permute-start.1 = (f32[512,1024]{1,0:T(8,128)}, f32[512,1024]{1,0:T(8,128)}, u32[]{:S(2)}, u32[]{:S(2)}) collective-permute-start(f32[512,1024]{1,0:T(8,128)} %get-tuple-element.62), channel_id=1, source_target_pairs={{0,1},{1,0},{2,3},{3,2},{4,5},{5,4},{6,7},{7,6},{8,9},{9,8},{10,11... | collective-permute-start | bytes 6291464 | tf_op jit(solution)/shard_map/ppermute | solution.py:691
  170.0 108.0 %collective-permute-start.2 = (f32[512,1024]{1,0:T(8,128)}, f32[512,1024]{1,0:T(8,128)}, u32[]{:S(2)}, u32[]{:S(2)}) collective-permute-start(f32[512,1024]{1,0:T(8,128)} %add.14), channel_id=1, source_target_pairs={{0,32},{1,33},{2,34},{3,35},{4,36},{5,37},{6,38},{7,39},{8,40},{9,... | collective-permute-start | bytes 6291464 | tf_op jit(solution)/shard_map/ppermute | solution.py:691
  208.7 69.3 %copy-start = (f32[512,1024]{1,0:T(8,128)S(1)}, f32[512,1024]{1,0:T(8,128)}, u32[]{:S(2)}) copy-start(f32[512,1024]{1,0:T(8,128)} %get-tuple-element.61) | copy-start | bytes 6291460
  275.2 9.9 %copy-start.2 = (bf16[256,1024]{1,0:T(8,128)(2,1)S(1)}, bf16[256,1024]{1,0:T(8,128)(2,1)}, u32[]{:S(2)}) copy-start(bf16[256,1024]{1,0:T(8,128)(2,1)} %reduce-scatter.2.cloned.1.call-done) | copy-start | bytes 1572868
  275.2 10.7 %copy-start.1 = (bf16[512,1024]{1,0:T(8,128)(2,1)S(1)}, bf16[512,1024]{1,0:T(8,128)(2,1)}, u32[]{:S(2)}) copy-start(bf16[512,1024]{1,0:T(8,128)(2,1)} %get-tuple-element.71) | copy-start | bytes 3145732
  276.3 10.6 %copy-start.3 = (bf16[128,1024]{1,0:T(8,128)(2,1)S(1)}, bf16[128,1024]{1,0:T(8,128)(2,1)}, u32[]{:S(2)}) copy-start(bf16[128,1024]{1,0:T(8,128)(2,1)} %get-tuple-element.72) | copy-start | bytes 786436
  276.3 8.8 %collective-permute-start.3 = (bf16[128,1024]{1,0:T(8,128)(2,1)S(1)}, bf16[128,1024]{1,0:T(8,128)(2,1)S(1)}, u32[]{:S(2)}, u32[]{:S(2)}) collective-permute-start(bf16[128,1024]{1,0:T(8,128)(2,1)S(1)} %slice.7), channel_id=1, source_target_pairs={{0,96},{1,97},{2,98},{3,99},{4,100},{5,101},{6,102},{7,103},{8,104... | collective-permute-start | bytes 786440 | tf_op jit(solution)/shard_map/ppermute | solution.py:691
Sparse Core Ops, SparseCore 0:
  10.1 72.2 all-gather.2
  89.9 49.4 all-gather.4
  142.8 90.8 reduce-scatter.1
